TPU v7x, 256 devices: a whole 4x4x8 slice. The times are simulated.
256 devices in a mesh: grp: 8 (over z_lo, y), dev: 32 (over z_hi, x, core).
Axes of the slice: x: 4, y: 4, z: 8 (z_hi: 4, z_lo: 2; z = z_hi * 2 + z_lo), core: 2. Of those that a mesh axis runs over, the one named last changes fastest.
Arguments:
- patch_features: bfloat16 [1024, 360448], P(None, ('grp', 'dev')), may hold values from -12 to 12
- upstream: bfloat16 [1024, 1024], P(('grp', 'dev')), may hold values from -115200 to 115200
Outputs:
- feature_grad: bfloat16 [1024, 360448], P(None, ('grp', 'dev'))
All inputs are finite; a program needn't handle non-finite values.
Results may differ from a plain program's by a relative error of at most 0.0051.
Values may be sent and summed in bfloat16 or wider, within the bound.
A program may use at most 64 MiB of HBM per device.

v0:
```python
import math

import jax
import jax.numpy as jnp
from jax import lax
from jax.sharding import PartitionSpec as P


def split_up(shard, dim, peers):
    before, after = (shard.shape[:dim], shard.shape[dim + 1 :])
    return jnp.moveaxis(shard.reshape(*before, peers, -1, *after), dim, 0)


def summed_on_arrival(shard, axis, dim):
    parts = split_up(shard, dim, lax.axis_size(axis))
    arrived = lax.all_to_all(parts, axis, split_axis=0, concat_axis=0, tiled=True)
    return arrived.sum(axis=0)


def sent_to_all(shard, axis):
    peers = lax.axis_size(axis)
    return lax.all_to_all(
        jnp.broadcast_to(shard[None], (peers, *shard.shape)), axis, 0, 0, tiled=True
    )


def joined_along(parts, dim):
    lengths = list(parts.shape[1:])
    lengths[dim] *= parts.shape[0]
    return jnp.moveaxis(parts, 0, dim).reshape(lengths)


def gather_directly(shard, axis, dim):
    parts = sent_to_all(shard, axis)
    return joined_along(parts, dim)


def on_device(patch_features, upstream):
    frames = patch_features.shape[0]
    feature_cols = patch_features.shape[1]
    group_count = lax.axis_size("grp")
    member_count = lax.axis_size("dev")
    scaling = 1.0 / math.sqrt(feature_cols * group_count * member_count)
    partial_sum = summed_on_arrival(
        lax.dot_general(
            patch_features,
            patch_features,
            (((1,), (1,)), ((), ())),
            preferred_element_type=jnp.float32,
        ),
        "grp",
        0,
    )
    products = summed_on_arrival(partial_sum, "dev", 0)
    own_rows = products.shape[0]
    row_offset = (lax.axis_index("grp") * member_count + lax.axis_index("dev")) * own_rows
    row_ids = row_offset + jnp.arange(own_rows, dtype=jnp.int32)[:, None]
    col_ids = jnp.arange(frames, dtype=jnp.int32)[None, :]
    scores = jnp.where(row_ids == col_ids, -jnp.inf, products * scaling)
    row_max = jnp.max(scores, axis=1, keepdims=True)
    exponent = jnp.exp(scores - row_max)
    weights = exponent / jnp.sum(exponent, axis=1, keepdims=True)
    upstream_f = upstream.astype(jnp.float32)
    weighted = jnp.sum(upstream_f * weights, axis=1, keepdims=True)
    score_grad = (scaling * weights * (upstream_f - weighted)).astype(jnp.bfloat16)
    gathered_dev = gather_directly(score_grad, "dev", 0)
    whole_grad = gather_directly(gathered_dev, "grp", 0)
    forward_part = jnp.dot(whole_grad, patch_features, preferred_element_type=jnp.float32)
    backward_part = lax.dot_general(
        whole_grad, patch_features, (((0,), (0,)), ((), ())), preferred_element_type=jnp.float32
    )
    return (forward_part + backward_part).astype(jnp.bfloat16)


def solution(mesh):
    return jax.shard_map(
        on_device,
        mesh=mesh,
        in_specs=(P(None, ("grp", "dev")), P(("grp", "dev"), None)),
        out_specs=P(None, ("grp", "dev")),
        check_vma=False,
    )
```

profile of v0, /device:TPU:1, one launch (start us, length us, event | category | flops | bytes accessed | tf_op | source)
XLA Modules:
  0.0 150.4 jit_solution(12975489729147052825)
XLA Ops:
  0.0 0.0 copy-start
  0.0 1.8 %copy-done = bf16[1024,1408]{1,0:T(8,128)(2,1)S(1)} copy-done((bf16[1024,1408]{1,0:T(8,128)(2,1)S(1)}, bf16[1024,1408]{1,0:T(8,128)(2,1)}, u32[]{:S(2)}) %copy-start) | copy-done | bytes 2883608
  1.8 3.4 %fusion.7 = f32[1024,1024]{1,0:T(8,128)S(1)} fusion(bf16[1024,1408]{1,0:T(8,128)(2,1)S(1)} %copy-done), kind=kOutput, calls=%fused_computation.13 | convolution fusion | flops 2952790016 | bytes 7077888 | tf_op jit(solution)/shard_map/dot_general | solution.py:45
  5.3 54.8 %all_to_all.20 = f32[8,128,1024]{2,1,0:T(8,128)} all-to-all(f32[8,128,1024]{2,1,0:T(8,128)S(1)} %bitcast.8), channel_id=1, replica_groups=mesh['grp'=8,'dev'=32] {'grp'}, dimensions={0} | all-to-all | bytes 8388608 | tf_op jit(solution)/shard_map/all_to_all | solution.py:16
  60.0 0.0 copy-start.1
  60.0 2.6 %reduce_sum.36 = f32[128,1024]{1,0:T(8,128)S(1)} reduce(f32[8,128,1024]{2,1,0:T(8,128)} %all_to_all.20, f32[]{:T(128)} %constant.17.clone.1), dimensions={0}, to_apply=%region_0.0 | reduce | flops 917504 | bytes 4718596 | tf_op jit(solution)/shard_map/reduce_sum | solution.py:17
  62.7 0.9 reshape.20
  63.6 12.6 %all-to-all-start.1 = ((f32[32,4,1024]{2,1,0:T(4,128)}), f32[32,4,1024]{2,1,0:T(4,128)S(1)}, u32[]{:S(2)}, u32[]{:S(2)}) async-start(f32[32,4,1024]{2,1,0:T(4,128)} %reshape.20), calls=%async_computation.1 | async-start | bytes 1048576 | tf_op jit(solution)/shard_map/all_to_all | solution.py:16
  76.2 18.4 %all-to-all-done.1 = f32[32,4,1024]{2,1,0:T(4,128)S(1)} async-done(((f32[32,4,1024]{2,1,0:T(4,128)}), f32[32,4,1024]{2,1,0:T(4,128)S(1)}, u32[]{:S(2)}, u32[]{:S(2)}) %all-to-all-start.1) | async-done | bytes 524320 | tf_op jit(solution)/shard_map/all_to_all | solution.py:16
  94.6 0.1 reduce_sum.37
  94.7 0.2 fusion.5
  94.9 0.2 fusion.4
  95.1 0.0 copy-done.1
  95.1 0.2 fusion
  95.3 0.1 fusion.2
  95.3 0.1 broadcast_in_dim.11
  95.4 17.4 %all_to_all.21 = bf16[32,4,1024]{2,1,0:T(4,128)(2,1)S(1)} all-to-all(bf16[32,4,1024]{2,1,0:T(4,128)(2,1)S(1)} %broadcast_in_dim.11), channel_id=1, replica_groups=mesh['grp'=8,'dev'=32] {'dev'}, dimensions={0} | all-to-all | bytes 524288 | tf_op jit(solution)/shard_map/all_to_all | solution.py:22
  112.9 0.1 broadcast_in_dim.12
  112.9 0.3 broadcast_in_dim.13
  113.2 28.8 %all_to_all.22 = bf16[8,128,1024]{2,1,0:T(8,128)(2,1)S(1)} all-to-all(bf16[8,128,1024]{2,1,0:T(8,128)(2,1)S(1)} %broadcast_in_dim.13), channel_id=1, replica_groups=mesh['grp'=8,'dev'=32] {'grp'}, dimensions={0} | all-to-all | bytes 4194304 | tf_op jit(solution)/shard_map/all_to_all | solution.py:22
  142.0 3.4 %fusion.8 = f32[1024,1408]{1,0:T(8,128)S(1)} fusion(bf16[1024,1024]{1,0:T(8,128)(2,1)S(1)} %bitcast.9, bf16[1024,1408]{1,0:T(8,128)(2,1)S(1)} %copy-done), kind=kOutput, calls=%fused_computation.14 | convolution fusion | flops 2952790016 | bytes 10747904 | tf_op jit(solution)/shard_map/dot_general | solution.py:68
  145.4 5.0 %add_convert_fusion = bf16[1024,1408]{1,0:T(8,128)(2,1)} fusion(f32[1024,1408]{1,0:T(8,128)S(1)} %fusion.8, bf16[1024,1024]{1,0:T(8,128)(2,1)S(1)} %bitcast.10, bf16[1024,1408]{1,0:T(8,128)(2,1)S(1)} %copy-done), kind=kOutput, calls=%fused_computation | convolution fusion | flops 2955673600 | bytes 13631488 | tf_op jit(solution)/shard_map/dot_general | solution.py:69
  (1 shorter events, 0.0 us)
Async XLA Ops:
  0.0 1.8 %copy-start = (bf16[1024,1408]{1,0:T(8,128)(2,1)S(1)}, bf16[1024,1408]{1,0:T(8,128)(2,1)}, u32[]{:S(2)}) copy-start(bf16[1024,1408]{1,0:T(8,128)(2,1)} %param.2) | copy-start | bytes 8650756
  60.0 35.0 %copy-start.1 = (bf16[4,1024]{1,0:T(4,128)(2,1)S(1)}, bf16[4,1024]{1,0:T(4,128)(2,1)}, u32[]{:S(2)}) copy-start(bf16[4,1024]{1,0:T(4,128)(2,1)} %param.3) | copy-start | bytes 24580
  63.6 31.0 %all-to-all-start.1 = ((f32[32,4,1024]{2,1,0:T(4,128)}), f32[32,4,1024]{2,1,0:T(4,128)S(1)}, u32[]{:S(2)}, u32[]{:S(2)}) async-start(f32[32,4,1024]{2,1,0:T(4,128)} %reshape.20), calls=%async_computation.1 | async-start | bytes 1048576 | tf_op jit(solution)/shard_map/all_to_all | solution.py:16
where the time goes:
time: 151 us; the launch traced here: 150 us
  blocking collectives  101 us (67%)
  waiting for transfers between devices  18.4 us (12%)
  starting transfers between devices  12.6 us (8%)
  matrix products  11.8 us (8%)
  other arithmetic  3.38 us (2%)
  local copies, waits for them, and re-layouts  3.15 us (2%)
    all_to_all x1, blocking collectives, summed_on_arrival(): lax.all_to_all(parts, axis, split_axis=0, concat_axis=0, tiled=True)  54.8 us
    all_to_all x2, blocking collectives, sent_to_all(): lax.all_to_all(jnp.broadcast_to(shard[None], (peers, *shard.shape)), axis...  46.2 us
    all_to_all x1, waiting for transfers between devices, summed_on_arrival(): lax.all_to_all(parts, axis, split_axis=0, concat_axis=0, tiled=True)  18.4 us
    all_to_all x1, starting transfers between devices, summed_on_arrival(): lax.all_to_all(parts, axis, split_axis=0, concat_axis=0, tiled=True)  12.6 us
    dot_general x1, matrix products, on_device(): lax.dot_general(whole_grad, patch_features, (((0,), (0,)), ((), ())), pre...  4.98 us
    dot_general x1, matrix products, on_device(): lax.dot_general(patch_features, patch_features, (((1,), (1,)), ((), ())),...  3.44 us
    dot_general x1, matrix products, on_device(): jnp.dot(whole_grad, patch_features, preferred_element_type=jnp.float32)  3.41 us
  transfers between devices with their start and end apart: 1, of which 1 were waited for; matrix products, arithmetic and copies ran while one was open for 0% of the time, Pallas kernels for 0%

commit v1 on v0

v1 whole, which is shorter than its diff:
```python
import functools
import math

import jax
import jax.numpy as jnp
from jax import lax
from jax.experimental import pallas as pl
from jax.experimental.pallas import tpu as pltpu
from jax.sharding import PartitionSpec as P

MESH = pl.DeviceIdType.MESH
WIRE = jnp.float32

NY, NX, NZ, NZL, NZH, CORES = 4, 4, 8, 2, 4, 2
NXY = NX * NY
CHIP_ROWS = 8
FRAMES = 1024
HALF = FRAMES // CORES
COLS_A = 384
COLS_B = HALF - COLS_A
BLOCK = 128


def comm_kernel(
    scale,
    p_ref,
    u_ref,
    w_ref,
    xs,
    xr,
    sa,
    ra,
    sb,
    rb,
    sa2,
    ra2,
    sb2,
    rb2,
    hs,
    hr,
    ub,
    ga1,
    gb1,
    ga,
    gb,
    sg,
    x_send, x_recv, a_send, a_recv, b_send, b_recv,
    a2_send, a2_recv, b2_send, b2_recv, h_sem, u_sem,
    ga1_send, ga1_recv, gb1_send, gb1_recv,
    ga_send, ga_recv, gb_send, gb_recv,
    fa_send, fa_recv, fb_send, fb_recv,
):
    g = lax.axis_index("grp")
    d = lax.axis_index("dev")
    z_lo, y = lax.div(g, NY), lax.rem(g, NY)
    core = lax.rem(d, CORES)
    x = lax.rem(lax.div(d, CORES), NX)
    z_hi = lax.div(d, CORES * NX)
    z = z_hi * NZL + z_lo
    my_xy = y * NX + x
    my_z = z_lo * NZH + z_hi
    partner = (g, d + 1 - 2 * core)

    def at_xy(yt, xt):
        return (z_lo * NY + yt, (z_hi * NX + xt) * CORES + core)

    def z_member(dz):
        zt = lax.rem(z + dz, NZ)
        return lax.rem(zt, NZL) * NZH + lax.div(zt, NZL)

    def at_z(dz):
        zt = lax.rem(z + dz, NZ)
        return (
            lax.rem(zt, NZL) * NY + y,
            (lax.div(zt, NZL) * NX + x) * CORES + core,
        )

    def xy_offset(k):
        return lax.rem(y + k // NX, NY), lax.rem(x + k % NX, NX)

    def remote(src, dst, send, recv, to):
        return pltpu.make_async_remote_copy(
            src_ref=src, dst_ref=dst, send_sem=send, recv_sem=recv,
            device_id=to, device_id_type=MESH,
        )

    barrier = pltpu.get_barrier_semaphore()
    pl.semaphore_signal(barrier, inc=1, device_id=partner, device_id_type=MESH)
    for k in range(1, NXY):
        pl.semaphore_signal(barrier, inc=1, device_id=at_xy(*xy_offset(k)), device_id_type=MESH)
    for dz in range(1, NZ):
        pl.semaphore_signal(barrier, inc=1, device_id=at_z(dz), device_id_type=MESH)

    theirs = pl.multiple_of((1 - core) * HALF, HALF)
    mine = pl.multiple_of(core * HALF, HALF)

    def product(row0, col0):
        return lax.dot_general(
            p_ref[pl.ds(row0, BLOCK), :],
            p_ref[pl.ds(col0, HALF), :],
            (((1,), (1,)), ((), ())),
            preferred_element_type=jnp.float32,
        )

    def order(i):
        yt = lax.rem(y + 1 + lax.div(i, NZL), NY)
        return lax.rem(i, NZL) * NY + yt

    def partner_order(i):
        return order(i)

    xs[0] = product(pl.multiple_of(partner_order(0) * BLOCK, BLOCK), theirs)
    pl.semaphore_wait(barrier, 1 + (NXY - 1) + (NZ - 1))
    u_copy = remote(u_ref, ub.at[core], u_sem.at[0], u_sem.at[1], partner)
    u_copy.start()
    ub[core] = u_ref[...]

    def x_copy(i):
        return remote(xs.at[i], xr.at[i], x_send.at[i], x_recv.at[i], partner)

    x_copy(0).start()

    @pl.loop(1, 8)
    def _(i):
        xs[i] = product(pl.multiple_of(partner_order(i) * BLOCK, BLOCK), theirs)
        x_copy(i).start()

    def a_copy(k, yt, xt):
        return remote(
            sa.at[yt * NX + xt], ra.at[k], a_send.at[k], a_recv.at[k], at_xy(yt, xt)
        )

    @pl.loop(0, 8)
    def _(i):
        block = order(i)
        zl, yt = lax.div(block, NY), lax.rem(block, NY)
        own = product(pl.multiple_of(block * BLOCK, BLOCK), mine)
        x_copy(i).wait_recv()
        total = (own + xr[i]).astype(WIRE)
        for zh in range(NZH):
            for xx in range(NX):
                piece = total[(zh * NX + xx) * CHIP_ROWS : (zh * NX + xx + 1) * CHIP_ROWS]
                sa[yt * NX + xx, zl * NZH + zh] = piece[:, :COLS_A]
                sb[zl * NZH + zh, yt * NX + xx] = piece[:, COLS_A:]

        @pl.when(lax.rem(i, NZL) == NZL - 1)
        def _():
            step = lax.div(i, NZL)
            for dx in range(NX):
                xt = lax.rem(x + dx, NX)

                @pl.when(jnp.logical_or(step < NY - 1, dx > 0))
                def _():
                    a_copy(step * NX + dx, yt, xt).start()

    def b_copy(dz):
        return remote(
            sb.at[z_member(dz)], rb.at[dz], b_send.at[dz], b_recv.at[dz], at_z(dz)
        )

    for dz in range(1, NZ):
        b_copy(dz).start()

    own_slot = (NY - 1) * NX
    a_slots = [k for k in range(NXY) if k != own_slot]
    for k in a_slots:
        a_copy(k, y, x).wait_recv()

    for zz in range(NZ):
        acc = sa[my_xy, zz].astype(jnp.float32)
        for k in a_slots:
            acc = acc + ra[k, zz].astype(jnp.float32)
        sa2[zz] = acc

    def a2_copy(dz):
        return remote(
            sa2.at[z_member(dz)], ra2.at[dz], a2_send.at[dz], a2_recv.at[dz], at_z(dz)
        )

    for dz in range(1, NZ):
        a2_copy(dz).start()

    for dz in range(1, NZ):
        b_copy(dz).wait_recv()

    for m in range(NXY):
        acc = sb[my_z, m].astype(jnp.float32)
        for dz in range(1, NZ):
            acc = acc + rb[dz, m].astype(jnp.float32)
        sb2[m] = acc

    def b2_copy(k):
        yt, xt = xy_offset(k)
        return remote(
            sb2.at[yt * NX + xt], rb2.at[k], b2_send.at[k], b2_recv.at[k], at_xy(yt, xt)
        )

    for k in range(1, NXY):
        b2_copy(k).start()

    for dz in range(1, NZ):
        a2_copy(dz).wait_recv()
    acc = sa2[my_z]
    for dz in range(1, NZ):
        acc = acc + ra2[dz]
    hs[:, :COLS_A] = acc
    for k in range(1, NXY):
        b2_copy(k).wait_recv()
    acc = sb2[my_xy]
    for k in range(1, NXY):
        acc = acc + rb2[k]
    hs[:, COLS_A:] = acc

    h_copy = remote(hs, hr, h_sem.at[0], h_sem.at[1], partner)
    h_copy.start()
    u_copy.wait_recv()
    h_copy.wait_recv()

    first = core == 0
    left = jnp.where(first, hs[...], hr[...])
    right = jnp.where(first, hr[...], hs[...])
    products = jnp.concatenate([left, right], axis=1)
    row0 = (((z_lo * NY + y) * NZH + z_hi) * NX + x) * CHIP_ROWS
    row_ids = row0 + lax.broadcasted_iota(jnp.int32, (CHIP_ROWS, FRAMES), 0)
    col_ids = lax.broadcasted_iota(jnp.int32, (CHIP_ROWS, FRAMES), 1)
    scores = jnp.where(row_ids == col_ids, -jnp.inf, products * scale)
    row_max = jnp.max(scores, axis=1, keepdims=True)
    exponent = jnp.exp(scores - row_max)
    weights = exponent / jnp.sum(exponent, axis=1, keepdims=True)
    up = jnp.concatenate(
        [ub[0].astype(jnp.float32), ub[1].astype(jnp.float32)], axis=0
    )
    weighted = jnp.sum(up * weights, axis=1, keepdims=True)
    score_grad = scale * weights * (up - weighted)
    own_cols = jnp.where(first, score_grad[:, :HALF], score_grad[:, HALF:])
    own_cols = own_cols.astype(jnp.bfloat16)
    ga1[my_z] = own_cols[:, :COLS_A]
    gb1[my_xy] = own_cols[:, COLS_A:]

    def ga1_copy(dz):
        return remote(
            ga1.at[my_z], ga1.at[my_z], ga1_send.at[dz], ga1_recv.at[dz], at_z(dz)
        )

    def gb1_copy(k):
        return remote(
            gb1.at[my_xy], gb1.at[my_xy], gb1_send.at[k], gb1_recv.at[k], at_xy(*xy_offset(k))
        )

    for k in range(1, NXY):
        gb1_copy(k).start()
    for dz in range(1, NZ):
        ga1_copy(dz).start()

    def ga_copy(k):
        return remote(
            ga1, ga.at[core, my_xy], ga_send.at[k], ga_recv.at[k], at_xy(*xy_offset(k))
        )

    def gb_copy(dz):
        return remote(
            gb1, gb.at[core, my_z], gb_send.at[dz], gb_recv.at[dz], at_z(dz)
        )

    def fa_copy(k):
        yt, xt = lax.rem(y + NY - k // NX, NY), lax.rem(x + NX - k % NX, NX)
        slot = ga.at[core, yt * NX + xt]
        return remote(slot, slot, fa_send.at[k], fa_recv.at[k], partner)

    def fb_copy(dz):
        slot = gb.at[core, z_member(NZ - dz)]
        return remote(slot, slot, fb_send.at[dz], fb_recv.at[dz], partner)

    for dz in range(1, NZ):
        ga1_copy(dz).wait_recv()
    for k in range(1, NXY):
        ga_copy(k).start()
    for k in range(1, NXY):
        gb1_copy(k).wait_recv()
    for dz in range(1, NZ):
        gb_copy(dz).start()
    ga[core, my_xy] = ga1[...]
    fa_copy(0).start()
    gb[core, my_z] = gb1[...]
    fb_copy(0).start()
    for k in range(1, NXY):
        ga_copy(k).wait_recv()
        fa_copy(k).start()
    for dz in range(1, NZ):
        gb_copy(dz).wait_recv()
        fb_copy(dz).start()
    for k in range(NXY):
        fa_copy(k).wait_recv()
    for dz in range(NZ):
        fb_copy(dz).wait_recv()

    @pl.loop(0, NZL * NY)
    def _(block):
        zl, yt = lax.div(block, NY), lax.rem(block, NY)
        for zh in range(NZH):
            for xx in range(NX):
                rows = pl.ds(
                    pl.multiple_of(block * BLOCK + (zh * NX + xx) * CHIP_ROWS, CHIP_ROWS),
                    CHIP_ROWS,
                )
                for c in range(CORES):
                    sg[rows, c * HALF : c * HALF + COLS_A] = ga[
                        c, yt * NX + xx, zl * NZH + zh
                    ].astype(jnp.float32)
                    sg[rows, c * HALF + COLS_A : (c + 1) * HALF] = gb[
                        c, zl * NZH + zh, yt * NX + xx
                    ].astype(jnp.float32)

    @pl.loop(0, 8)
    def _(bi):
        ri = pl.ds(pl.multiple_of(bi * BLOCK, BLOCK), BLOCK)
        for bj in range(8):
            cj = pl.ds(bj * BLOCK, BLOCK)
            w_ref[ri, cj] = (sg[ri, cj] + sg[cj, ri].T).astype(jnp.bfloat16)

    u_copy.wait_send()
    h_copy.wait_send()
    for i in range(8):
        x_copy(i).wait_send()
    for k in a_slots:
        a_copy(k, y, x).wait_send()
    for k in range(1, NXY):
        b2_copy(k).wait_send()
        gb1_copy(k).wait_send()
        ga_copy(k).wait_send()
    for dz in range(1, NZ):
        b_copy(dz).wait_send()
        a2_copy(dz).wait_send()
        ga1_copy(dz).wait_send()
        gb_copy(dz).wait_send()
    for k in range(NXY):
        fa_copy(k).wait_send()
    for dz in range(NZ):
        fb_copy(dz).wait_send()


def grad_weights(patch_features, upstream, scale):
    dma = lambda n: pltpu.SemaphoreType.DMA((n,))
    f32, bf16 = jnp.float32, jnp.bfloat16
    return pl.pallas_call(
        functools.partial(comm_kernel, scale),
        out_shape=jax.ShapeDtypeStruct((FRAMES, FRAMES), bf16),
        in_specs=[pl.BlockSpec(memory_space=pltpu.VMEM)] * 2,
        out_specs=pl.BlockSpec(memory_space=pltpu.VMEM),
        scratch_shapes=[
            pltpu.VMEM((8, BLOCK, HALF), f32),
            pltpu.VMEM((8, BLOCK, HALF), f32),
            pltpu.VMEM((NXY, NZ, CHIP_ROWS, COLS_A), WIRE),
            pltpu.VMEM((NXY, NZ, CHIP_ROWS, COLS_A), WIRE),
            pltpu.VMEM((NZ, NXY, CHIP_ROWS, COLS_B), WIRE),
            pltpu.VMEM((NZ, NXY, CHIP_ROWS, COLS_B), WIRE),
            pltpu.VMEM((NZ, CHIP_ROWS, COLS_A), f32),
            pltpu.VMEM((NZ, CHIP_ROWS, COLS_A), f32),
            pltpu.VMEM((NXY, CHIP_ROWS, COLS_B), f32),
            pltpu.VMEM((NXY, CHIP_ROWS, COLS_B), f32),
            pltpu.VMEM((CHIP_ROWS, HALF), f32),
            pltpu.VMEM((CHIP_ROWS, HALF), f32),
            pltpu.VMEM((CORES, 4, FRAMES), bf16),
            pltpu.VMEM((NZ, CHIP_ROWS, COLS_A), bf16),
            pltpu.VMEM((NXY, CHIP_ROWS, COLS_B), bf16),
            pltpu.VMEM((CORES, NXY, NZ, CHIP_ROWS, COLS_A), bf16),
            pltpu.VMEM((CORES, NZ, NXY, CHIP_ROWS, COLS_B), bf16),
            pltpu.VMEM((FRAMES, FRAMES), f32),
            dma(8), dma(8), dma(NXY), dma(NXY), dma(NZ), dma(NZ),
            dma(NZ), dma(NZ), dma(NXY), dma(NXY), dma(2), dma(2),
            dma(NZ), dma(NZ), dma(NXY), dma(NXY),
            dma(NXY), dma(NXY), dma(NZ), dma(NZ),
            dma(NXY), dma(NXY), dma(NZ), dma(NZ),
        ],
        compiler_params=pltpu.CompilerParams(
            collective_id=0, has_side_effects=True, vmem_limit_bytes=48 * 1024 * 1024
        ),
    )(patch_features, upstream)


def on_device(patch_features, upstream):
    features = patch_features.shape[1] * lax.axis_size("grp") * lax.axis_size("dev")
    sym = grad_weights(patch_features, upstream, 1.0 / math.sqrt(features))
    return jnp.dot(sym, patch_features, preferred_element_type=jnp.float32).astype(jnp.bfloat16)


def solution(mesh):
    return jax.shard_map(
        on_device,
        mesh=mesh,
        in_specs=(P(None, ("grp", "dev")), P(("grp", "dev"), None)),
        out_specs=P(None, ("grp", "dev")),
        check_vma=False,
    )
```

time: 151 us -> 75.2 us (0.50)
  blocking collectives: 101 us -> 0 us
  Pallas kernels: 0 us -> 67.8 us
  waiting for transfers between devices: 18.4 us -> 0 us
  starting transfers between devices: 12.6 us -> 0 us
  matrix products: 11.8 us -> 4.73 us
  other arithmetic: 3.38 us -> 0 us
    all_to_all x3 -> x0, blocking collectives: 101 us -> none  [the longest x1 54.8 us: summed_on_arrival(): lax.all_to_all(parts, axis, split_axis=0, concat_axis=0, tiled=True)]
    pallas_call x0 -> x1, Pallas kernels: none -> 67.8 us  [grad_weights(): pl.pallas_call(functools.partial(comm_kernel, scale), out_shape=jax.Shape...]
    all_to_all x1 -> x0, waiting for transfers between devices: 18.4 us -> none  [summed_on_arrival(): lax.all_to_all(parts, axis, split_axis=0, concat_axis=0, tiled=True)]
    all_to_all x1 -> x0, starting transfers between devices: 12.6 us -> none  [summed_on_arrival(): lax.all_to_all(parts, axis, split_axis=0, concat_axis=0, tiled=True)]
    dot_general x3 -> x1, matrix products: 11.8 us -> 4.73 us  [on_device(): jnp.dot(sym, patch_features, preferred_element_type=jnp.float32)]
    reduce_sum x4 -> x0, other arithmetic: 3.11 us -> none  [the longest x2 2.71 us: summed_on_arrival(): return arrived.sum(axis=0)]
  transfers between devices with their start and end apart: 1 -> 0, of which waited for: 1 -> 0; matrix products, arithmetic and copies ran while one was open for 0% -> 0% of each run, Pallas kernels for 0% -> 0%
where the time goes in v1:
time: 75.2 us; the launch traced here: 75.1 us
  Pallas kernels  67.8 us (90%)
  matrix products  4.73 us (6%)
  local copies, waits for them, and re-layouts  2.51 us (3%)
    pallas_call x1, Pallas kernels, grad_weights(): pl.pallas_call(functools.partial(comm_kernel, scale), out_shape=jax.Shape...  67.8 us
    dot_general x1, matrix products, on_device(): jnp.dot(sym, patch_features, preferred_element_type=jnp.float32)  4.73 us
    unnamed x4, local copies, waits for them, and re-layouts  2.51 us

profile of v1, /device:TPU:1, one launch (start us, length us, event | category | flops | bytes accessed | tf_op | source)
XLA Modules:
  0.0 75.1 jit_solution(187742776653090095)
XLA Ops:
  0.0 0.0 copy-start
  0.0 1.8 %copy-done = bf16[1024,1408]{1,0:T(8,128)(2,1)S(1)} copy-done((bf16[1024,1408]{1,0:T(8,128)(2,1)S(1)}, bf16[1024,1408]{1,0:T(8,128)(2,1)}, u32[]{:S(2)}) %copy-start) | copy-done | bytes 2883608
  1.8 0.0 copy-start.1
  1.8 0.7 copy-done.1
  2.5 67.8 %shard_map.28 = bf16[1024,1024]{1,0:T(8,128)(2,1)S(1)} custom-call(bf16[1024,1408]{1,0:T(8,128)(2,1)S(1)} %copy-done, bf16[4,1024]{1,0:T(4,128)(2,1)S(1)} %copy-done.1), custom_call_target="tpu_custom_call" | custom-call | tf_op jit(solution)/shard_map/pallas_call | solution.py:345
  70.4 4.7 %convolution_convert_fusion = bf16[1024,1408]{1,0:T(8,128)(2,1)} fusion(bf16[1024,1024]{1,0:T(8,128)(2,1)S(1)} %shard_map.28, bf16[1024,1408]{1,0:T(8,128)(2,1)S(1)} %copy-done), kind=kOutput, calls=%fused_computation | convolution fusion | flops 2954231808 | bytes 7864320 | tf_op jit(solution)/shard_map/dot_general | solution.py:384
Async XLA Ops:
  0.0 1.8 %copy-start = (bf16[1024,1408]{1,0:T(8,128)(2,1)S(1)}, bf16[1024,1408]{1,0:T(8,128)(2,1)}, u32[]{:S(2)}) copy-start(bf16[1024,1408]{1,0:T(8,128)(2,1)} %p_ref.1) | copy-start | bytes 8650756
  1.8 0.7 copy-start.1

commit v2 on v0

v2 whole, which is shorter than its diff:
```python
import functools
import math

import jax
import jax.numpy as jnp
from jax import lax
from jax.experimental import pallas as pl
from jax.experimental.pallas import tpu as pltpu
from jax.sharding import PartitionSpec as P

MESH = pl.DeviceIdType.MESH
WIRE = jnp.float32

NY, NX, NZ, NZL, NZH, CORES = 4, 4, 8, 2, 4, 2
NXY = NX * NY
CHIP_ROWS = 8
FRAMES = 1024
HALF = FRAMES // CORES
COLS_A = 384
COLS_B = HALF - COLS_A
RUN = NX * CHIP_ROWS
PAIRS = NZ // 2
FAR = NZ // 2
BLOCK = 2 * NY * RUN
TILE = 128
ROWS = 256


def comm_kernel(
    scale,
    p_hbm,
    u_hbm,
    sg,
    p_ref,
    xs,
    xr,
    sa,
    ra,
    sm,
    rm,
    sb,
    rb,
    sa2,
    ra2,
    sb2,
    rb2,
    rf,
    sf,
    hs,
    hr,
    ub,
    ga,
    gb,
    p_sem, u_in, f_sem, e_sem,
    x_send, x_recv, a_send, a_recv, m_send, m_recv, b_send, b_recv,
    a2_send, a2_recv, b2_send, b2_recv, h_sem, u_sem,
    gaz_send, gaz_recv, gbp_send, gbp_recv,
    ga1_send, ga1_recv, ga2_send, ga2_recv, gbz_send, gbz_recv,
    fa_send, fa_recv, fb_send, fb_recv,
):
    p_load = pltpu.make_async_copy(p_hbm, p_ref, p_sem.at[0])
    p_load.start()
    g = lax.axis_index("grp")
    d = lax.axis_index("dev")
    z_lo, y = lax.div(g, NY), lax.rem(g, NY)
    core = lax.rem(d, CORES)
    x = lax.rem(lax.div(d, CORES), NX)
    z_hi = lax.div(d, CORES * NX)
    z = z_hi * NZL + z_lo
    my_xy = y * NX + x
    partner = (g, d + 1 - 2 * core)
    u_load = pltpu.make_async_copy(u_hbm, ub.at[core], u_in.at[0])
    u_load.start()

    ys = [lax.rem(y + dy, NY) for dy in range(NY)]
    xs_ = [lax.rem(x + dx, NX) for dx in range(NX)]
    xy_at = []
    xy_slot = []
    for k in range(NXY):
        yt, xt = ys[k // NX], xs_[k % NX]
        xy_at.append((z_lo * NY + yt, (z_hi * NX + xt) * CORES + core))
        xy_slot.append(yt * NX + xt)

    def ring(n):
        return min(n, 4 - n)

    far_first = sorted(range(1, NXY), key=lambda k: -ring(k // NX) - ring(k % NX))

    def z_plus(dz):
        return lax.rem(z + dz, NZ)

    def at_z(dz):
        zt = z_plus(dz)
        return (
            lax.rem(zt, NZL) * NY + y,
            (lax.div(zt, NZL) * NX + x) * CORES + core,
        )

    def remote(src, dst, send, recv, to):
        return pltpu.make_async_remote_copy(
            src_ref=src, dst_ref=dst, send_sem=send, recv_sem=recv,
            device_id=to, device_id_type=MESH,
        )

    def arrived(whole, sem):
        remote(whole, whole, sem, sem, partner).wait_recv()

    def sent(whole, sem):
        remote(whole, whole, sem, sem, partner).wait_send()

    barrier = pltpu.get_barrier_semaphore()
    for dz in (4, 3, 5, 2, 6, 1, 7):
        pl.semaphore_signal(barrier, inc=1, device_id=at_z(dz), device_id_type=MESH)
    for k in reversed(range(1, NXY)):
        pl.semaphore_signal(barrier, inc=1, device_id=xy_at[k], device_id_type=MESH)
    pl.semaphore_signal(barrier, inc=1, device_id=partner, device_id_type=MESH)

    theirs = pl.multiple_of((1 - core) * HALF, HALF)
    mine = pl.multiple_of(core * HALF, HALF)

    def product(i, col0):
        runs = []
        for dz in (4 + i, 3 - i):
            zt = z_plus(dz)
            for yy in range(NY):
                row = lax.rem(zt, NZL) * (FRAMES // NZL) + yy * (FRAMES // (NZL * NY)) + lax.div(zt, NZL) * RUN
                runs.append(p_ref[pl.ds(pl.multiple_of(row, RUN), RUN), :])
        return lax.dot_general(
            jnp.concatenate(runs, axis=0),
            p_ref[pl.ds(col0, HALF), :],
            (((1,), (1,)), ((), ())),
            preferred_element_type=jnp.float32,
        )

    def x_copy(i):
        return remote(xs.at[i], xr.at[i], x_send.at[0], x_recv.at[i], partner)

    p_load.wait()
    xs[0] = product(0, theirs)
    u_load.wait()
    pl.semaphore_wait(barrier, 1 + (NXY - 1) + (NZ - 1))
    x_copy(0).start()
    u_copy = remote(ub.at[core], ub.at[core], u_sem.at[0], u_sem.at[1], partner)
    u_copy.start()

    @pl.loop(1, PAIRS)
    def _(i):
        xs[i] = product(i, theirs)
        x_copy(i).start()

    def first_axis(i, n):
        return (ys[n], xy_at[n * NX]) if i % 2 == 0 else (xs_[n], xy_at[n])

    def second_axis(i, n):
        return first_axis(i + 1, n)

    def a_copy(i, n):
        index, to = first_axis(i, n)
        return remote(sa.at[i, index], ra.at[i, n], a_send.at[0], a_recv.at[i], to)

    def m_copy(i, n):
        index, to = second_axis(i, n)
        return remote(sm.at[i, index], rm.at[i, n], m_send.at[0], m_recv.at[i], to)

    def b_copy(i, s):
        dz = 4 + i if s == 0 else 3 - i
        return remote(sb.at[i, s], rb.at[dz], b_send.at[0], b_recv.at[0], at_z(dz))

    def f_copy(k):
        return remote(sb.at[0, 0, xy_slot[k]], rf.at[k], f_sem.at[0], f_sem.at[1], xy_at[k])

    f2_copy = remote(sf.at[0], sf.at[1], f_sem.at[2], f_sem.at[3], at_z(FAR))

    for i in range(PAIRS):
        own = product(i, mine)
        x_copy(i).wait_recv()
        total = own + xr[i]
        for s in range(2):
            for m in range(NXY):
                row = (s * NXY + m) * CHIP_ROWS
                piece = total[row : row + CHIP_ROWS].astype(WIRE)
                index = (m // NX, m % NX) if i % 2 == 0 else (m % NX, m // NX)
                sa[i, index[0], index[1], s] = piece[:, :COLS_A]
                sb[i, s, m] = piece[:, COLS_A:]
        if i == 0:
            for k in far_first:
                f_copy(k).start()
        else:
            b_copy(i, 0).start()
        for n in (2, 1, 3):
            a_copy(i, n).start()
        if i < PAIRS - 1:
            b_copy(i, 1).start()

    def a2_copy(i, s):
        dz = 4 + i if s == 0 else 3 - i
        return remote(sa2.at[i, s], ra2.at[dz], a2_send.at[0], a2_recv.at[0], at_z(dz))

    def sum_first(i):
        arrived(ra.at[i, pl.ds(1, NY - 1)], a_recv.at[i])
        own = first_axis(i, 0)[0]
        for j in range(NX):
            for s in range(2):
                acc = sa[i, own, j, s].astype(jnp.float32)
                for n in range(1, NY):
                    acc = acc + ra[i, n, j, s].astype(jnp.float32)
                sm[i, j, s] = acc
        for n in (2, 1, 3):
            m_copy(i, n).start()

    def sum_second(i):
        arrived(rm.at[i, pl.ds(1, NX - 1)], m_recv.at[i])
        own = second_axis(i, 0)[0]
        for s in range(2):
            acc = sm[i, own, s]
            for n in range(1, NX):
                acc = acc + rm[i, n, s]
            sa2[i, s] = acc
        a2_copy(i, 0).start()
        if i < PAIRS - 1:
            a2_copy(i, 1).start()

    def b2_copy(k):
        return remote(
            sb2.at[xy_slot[k]], rb2.at[k], b2_send.at[0], b2_recv.at[0], xy_at[k]
        )

    sum_first(0)
    sum_first(1)
    sum_first(2)
    arrived(rf.at[pl.ds(1, NXY - 1)], f_sem.at[1])
    acc = sb[0, 0, my_xy].astype(jnp.float32)
    for k in range(1, NXY):
        acc = acc + rf[k].astype(jnp.float32)
    sf[0] = acc
    f2_copy.start()

    arrived(rb.at[pl.ds(1, NZ - 2)], b_recv.at[0])
    for m in range(NXY):
        acc = sb[PAIRS - 1, 1, m].astype(jnp.float32)
        for dz in (1, 2, 3, 5, 6, 7):
            acc = acc + rb[dz, m].astype(jnp.float32)
        sb2[m] = acc
    for k in far_first:
        b2_copy(k).start()
    sum_first(3)
    for i in range(PAIRS):
        sum_second(i)

    arrived(rb2.at[pl.ds(1, NXY - 1)], b2_recv.at[0])
    acc = sb2[my_xy]
    for k in range(1, NXY):
        acc = acc + rb2[k]
    f2_copy.wait_recv()
    hs[:, COLS_A:] = acc + sf[1]
    arrived(ra2.at[pl.ds(1, NZ - 1)], a2_recv.at[0])
    acc = sa2[PAIRS - 1, 1]
    for dz in range(1, NZ):
        acc = acc + ra2[dz]
    hs[:, :COLS_A] = acc

    h_copy = remote(hs, hr, h_sem.at[0], h_sem.at[1], partner)
    h_copy.start()
    u_copy.wait_recv()
    up = jnp.concatenate(
        [ub[0].astype(jnp.float32), ub[1].astype(jnp.float32)], axis=0
    )
    h_copy.wait_recv()

    first = core == 0
    left = jnp.where(first, hs[...], hr[...])
    right = jnp.where(first, hr[...], hs[...])
    products = jnp.concatenate([left, right], axis=1)
    row0 = z_lo * (FRAMES // NZL) + y * (FRAMES // (NZL * NY)) + z_hi * RUN + x * CHIP_ROWS
    row_ids = row0 + lax.broadcasted_iota(jnp.int32, (CHIP_ROWS, FRAMES), 0)
    col_ids = lax.broadcasted_iota(jnp.int32, (CHIP_ROWS, FRAMES), 1)
    scores = jnp.where(row_ids == col_ids, -jnp.inf, products * scale)
    row_max = jnp.max(scores, axis=1, keepdims=True)
    exponent = jnp.exp(scores - row_max)
    weights = exponent / jnp.sum(exponent, axis=1, keepdims=True)
    weighted = jnp.sum(up * weights, axis=1, keepdims=True)
    score_grad = scale * weights * (up - weighted)
    own_cols = jnp.where(first, score_grad[:, :HALF], score_grad[:, HALF:])
    own_cols = own_cols.astype(jnp.bfloat16)
    ga[core, z, y, x] = own_cols[:, :COLS_A]
    gb[core, z, y, x] = own_cols[:, COLS_A:]

    def gaz_copy(dz):
        slot = ga.at[core, z, y, x]
        return remote(slot, slot, gaz_send.at[0], gaz_recv.at[dz], at_z(dz))

    def ga1_copy(dz, n):
        slot = ga.at[core, z_plus(NZ - dz), y, x]
        to = xy_at[n] if dz % 2 == 0 else xy_at[n * NX]
        return remote(slot, slot, ga1_send.at[0], ga1_recv.at[dz], to)

    def ga2_copy(dz, n):
        if dz % 2 == 0:
            slot, to = ga.at[core, z_plus(NZ - dz), y], xy_at[n * NX]
        else:
            slot, to = ga.at[core, z_plus(NZ - dz), :, x], xy_at[n]
        return remote(slot, slot, ga2_send.at[0], ga2_recv.at[dz], to)

    def gbp_copy(k):
        slot = gb.at[core, z, y, x]
        return remote(slot, slot, gbp_send.at[0], gbp_recv.at[k // NX], xy_at[k])

    def gbz_copy(dz, dy):
        slot = gb.at[core, z, ys[(NY - dy) % NY]]
        return remote(slot, slot, gbz_send.at[0], gbz_recv.at[dz], at_z(dz))

    def fa_copy(dz):
        slot = ga.at[core, z_plus(NZ - dz)]
        return remote(slot, slot, fa_send.at[0], fa_recv.at[dz], partner)

    def fb_copy(dz):
        slot = gb.at[core, z_plus(NZ - dz)]
        return remote(slot, slot, fb_send.at[0], fb_recv.at[dz], partner)

    own_b = gb.at[core, z, y, x]
    e_copy = remote(own_b, own_b, e_sem.at[0], e_sem.at[1], at_z(FAR))

    def e2_copy(k):
        slot = gb.at[core, z_plus(FAR), y, x]
        return remote(slot, slot, e_sem.at[2], gbz_recv.at[FAR], xy_at[k])

    z_order = (3, 5, 2, 6, 1, 7)
    gaz_copy(FAR).start()
    e_copy.start()
    for dz in z_order:
        gaz_copy(dz).start()
    for k in far_first:
        gbp_copy(k).start()

    def spread_1(dz):
        if dz:
            gaz_copy(dz).wait_recv()
        for n in (2, 1, 3):
            ga1_copy(dz, n).start()

    def spread_2(dz):
        arrived(ga.at[core, z, 0, pl.ds(0, 3)], ga1_recv.at[dz])
        for n in (2, 1, 3):
            ga2_copy(dz, n).start()

    def spread_b(dy):
        count = NX if dy else NX - 1
        arrived(gb.at[core, z, 0, pl.ds(0, count)], gbp_recv.at[dy])
        for dz in z_order:
            gbz_copy(dz, dy).start()

    spread_1(0)
    spread_1(1)
    spread_1(7)
    spread_2(0)
    spread_b(0)
    spread_1(2)
    spread_1(6)
    spread_b(1)
    spread_b(3)
    spread_2(1)
    spread_2(7)
    spread_1(3)
    spread_1(5)
    spread_b(2)
    spread_1(4)
    e_copy.wait_recv()
    for k in far_first:
        e2_copy(k).start()
    spread_2(2)
    spread_2(6)
    spread_2(3)
    spread_2(5)
    spread_2(4)

    def collect(dz):
        arrived(ga.at[core, pl.ds(0, 1), pl.ds(0, 3)], ga2_recv.at[dz])
        fa_copy(dz).start()
        if dz == FAR:
            arrived(gb.at[core, pl.ds(0, 5), 0, pl.ds(0, 3)], gbz_recv.at[dz])
        elif dz:
            arrived(gb.at[core, z], gbz_recv.at[dz])
        fb_copy(dz).start()

    def place(dz):
        fa_copy(dz).wait_recv()
        fb_copy(dz).wait_recv()
        zt = z_plus(NZ - dz)
        for yy in range(NY):
            base = lax.rem(zt, NZL) * (FRAMES // NZL) + yy * (FRAMES // (NZL * NY)) + lax.div(zt, NZL) * RUN
            for xx in range(NX):
                rows = pl.ds(pl.multiple_of(base + xx * CHIP_ROWS, CHIP_ROWS), CHIP_ROWS)
                for c in range(CORES):
                    sg[rows, c * HALF : c * HALF + COLS_A] = ga[
                        c, zt, yy, xx
                    ]
                    sg[rows, c * HALF + COLS_A : (c + 1) * HALF] = gb[
                        c, zt, yy, xx
                    ]

    order = (0, 1, 7, 2, 6, 3, 5, 4)
    for n, dz in enumerate(order):
        collect(dz)
        if n:
            place(order[n - 1])
    place(order[-1])

    u_copy.wait_send()
    h_copy.wait_send()
    sent(xs, x_send.at[0])
    sent(sa.at[:, pl.ds(1, NY - 1)], a_send.at[0])
    sent(sm.at[:, pl.ds(1, NX - 1)], m_send.at[0])
    sent(rb.at[pl.ds(1, NZ - 2)], b_send.at[0])
    sent(rf.at[pl.ds(1, NXY - 1)], f_sem.at[0])
    f2_copy.wait_send()
    sent(ra2.at[pl.ds(1, NZ - 1)], a2_send.at[0])
    sent(rb2.at[pl.ds(1, NXY - 1)], b2_send.at[0])
    sent(ga.at[0, pl.ds(1, NZ - 1), 0, 0], gaz_send.at[0])
    sent(gb.at[0, pl.ds(0, 5), 0, pl.ds(0, 3)], gbp_send.at[0])
    sent(ga.at[0, pl.ds(0, 2), pl.ds(0, 3)], ga1_send.at[0])
    sent(ga.at[0, pl.ds(0, 6)], ga2_send.at[0])
    sent(gb.at[0, pl.ds(1, NZ - 2)], gbz_send.at[0])
    e_copy.wait_send()
    sent(gb.at[0, pl.ds(0, 5), 0, pl.ds(0, 3)], e_sem.at[2])
    sent(ga.at[0], fa_send.at[0])
    sent(gb.at[0], fb_send.at[0])


def sum_kernel(g_ref, p_ref, o_hbm, out, sem):
    copies = []
    for i in range(FRAMES // ROWS):
        rows = slice(i * ROWS, (i + 1) * ROWS)
        tiles = []
        for j in range(FRAMES // TILE):
            cols = slice(j * TILE, (j + 1) * TILE)
            flipped = g_ref[cols, rows].T
            total = g_ref[rows, cols].astype(jnp.float32) + flipped.astype(jnp.float32)
            tiles.append(total.astype(jnp.bfloat16))
        out[i] = jnp.dot(
            jnp.concatenate(tiles, axis=1), p_ref[...], preferred_element_type=jnp.float32
        ).astype(jnp.bfloat16)
        copy = pltpu.make_async_copy(out.at[i], o_hbm.at[pl.ds(i * ROWS, ROWS)], sem.at[i])
        copy.start()
        copies.append(copy)
    for copy in copies:
        copy.wait()


def symmetric_product(score_grad, patch_features):
    shape = patch_features.shape
    blocks = FRAMES // ROWS
    return pl.pallas_call(
        sum_kernel,
        out_shape=jax.ShapeDtypeStruct(shape, jnp.bfloat16),
        in_specs=[pl.BlockSpec(memory_space=pltpu.VMEM)] * 2,
        out_specs=pl.BlockSpec(memory_space=pltpu.HBM),
        scratch_shapes=[
            pltpu.VMEM((blocks, ROWS, shape[1]), jnp.bfloat16),
            pltpu.SemaphoreType.DMA((blocks,)),
        ],
        compiler_params=pltpu.CompilerParams(vmem_limit_bytes=24 * 1024 * 1024),
    )(score_grad, patch_features)


def grad_weights(patch_features, upstream, scale):
    dma = lambda *n: pltpu.SemaphoreType.DMA(n)
    f32, bf16 = jnp.float32, jnp.bfloat16
    return pl.pallas_call(
        functools.partial(comm_kernel, scale),
        out_shape=jax.ShapeDtypeStruct((FRAMES, FRAMES), bf16),
        in_specs=[pl.BlockSpec(memory_space=pltpu.HBM)] * 2,
        out_specs=pl.BlockSpec(memory_space=pltpu.VMEM),
        scratch_shapes=[
            pltpu.VMEM(patch_features.shape, bf16),
            pltpu.VMEM((PAIRS, BLOCK, HALF), f32),
            pltpu.VMEM((PAIRS, BLOCK, HALF), f32),
            pltpu.VMEM((PAIRS, NY, NX, 2, CHIP_ROWS, COLS_A), WIRE),
            pltpu.VMEM((PAIRS, NY, NX, 2, CHIP_ROWS, COLS_A), WIRE),
            pltpu.VMEM((PAIRS, NX, 2, CHIP_ROWS, COLS_A), f32),
            pltpu.VMEM((PAIRS, NX, 2, CHIP_ROWS, COLS_A), f32),
            pltpu.VMEM((PAIRS, 2, NXY, CHIP_ROWS, COLS_B), WIRE),
            pltpu.VMEM((NZ, NXY, CHIP_ROWS, COLS_B), WIRE),
            pltpu.VMEM((PAIRS, 2, CHIP_ROWS, COLS_A), f32),
            pltpu.VMEM((NZ, CHIP_ROWS, COLS_A), f32),
            pltpu.VMEM((NXY, CHIP_ROWS, COLS_B), f32),
            pltpu.VMEM((NXY, CHIP_ROWS, COLS_B), f32),
            pltpu.VMEM((NXY, CHIP_ROWS, COLS_B), WIRE),
            pltpu.VMEM((2, CHIP_ROWS, COLS_B), f32),
            pltpu.VMEM((CHIP_ROWS, HALF), f32),
            pltpu.VMEM((CHIP_ROWS, HALF), f32),
            pltpu.VMEM((CORES, 4, FRAMES), bf16),
            pltpu.VMEM((CORES, NZ, NY, NX, CHIP_ROWS, COLS_A), bf16),
            pltpu.VMEM((CORES, NZ, NY, NX, CHIP_ROWS, COLS_B), bf16),
            dma(1), dma(1), dma(4), dma(3),
            dma(1), dma(PAIRS), dma(1), dma(PAIRS), dma(1), dma(PAIRS), dma(1), dma(1),
            dma(1), dma(1), dma(1), dma(1), dma(2), dma(2),
            dma(1), dma(NZ), dma(1), dma(NY),
            dma(1), dma(NZ), dma(1), dma(NZ), dma(1), dma(NZ),
            dma(1), dma(NZ), dma(1), dma(NZ),
        ],
        compiler_params=pltpu.CompilerParams(
            collective_id=0, has_side_effects=True, vmem_limit_bytes=40 * 1024 * 1024
        ),
    )(pltpu.with_memory_space_constraint(patch_features, pltpu.HBM), pltpu.with_memory_space_constraint(upstream, pltpu.HBM))


def on_device(patch_features, upstream):
    features = patch_features.shape[1] * lax.axis_size("grp") * lax.axis_size("dev")
    score_grad = grad_weights(patch_features, upstream, 1.0 / math.sqrt(features))
    return symmetric_product(score_grad, patch_features)


def solution(mesh):
    return jax.shard_map(
        on_device,
        mesh=mesh,
        in_specs=(P(None, ("grp", "dev")), P(("grp", "dev"), None)),
        out_specs=P(None, ("grp", "dev")),
        check_vma=False,
    )
```

time: 151 us -> 55.2 us (0.37)
  blocking collectives: 101 us -> 0 us
  Pallas kernels: 0 us -> 55.1 us
  waiting for transfers between devices: 18.4 us -> 0 us
  starting transfers between devices: 12.6 us -> 0 us
  matrix products: 11.8 us -> 0 us
  other arithmetic: 3.38 us -> 0 us
  local copies, waits for them, and re-layouts: 3.15 us -> 0.01 us
    all_to_all x3 -> x0, blocking collectives: 101 us -> none  [the longest x1 54.8 us: summed_on_arrival(): lax.all_to_all(parts, axis, split_axis=0, concat_axis=0, tiled=True)]
    pallas_call x0 -> x2, Pallas kernels: none -> 55.1 us  [the longest x1 50.7 us: grad_weights(): pl.pallas_call(functools.partial(comm_kernel, scale), out_shape=jax.Shape...]
    all_to_all x1 -> x0, waiting for transfers between devices: 18.4 us -> none  [summed_on_arrival(): lax.all_to_all(parts, axis, split_axis=0, concat_axis=0, tiled=True)]
    all_to_all x1 -> x0, starting transfers between devices: 12.6 us -> none  [summed_on_arrival(): lax.all_to_all(parts, axis, split_axis=0, concat_axis=0, tiled=True)]
    dot_general x3 -> x0, matrix products: 11.8 us -> none  [the longest x1 4.98 us: on_device(): lax.dot_general(whole_grad, patch_features, (((0,), (0,)), ((), ())), pre...]
    reduce_sum x4 -> x0, other arithmetic: 3.11 us -> none  [the longest x2 2.71 us: summed_on_arrival(): return arrived.sum(axis=0)]
    unnamed x4 -> x2, local copies, waits for them, and re-layouts: 1.82 us -> 0.01 us
  transfers between devices with their start and end apart: 1 -> 0, of which waited for: 1 -> 0; matrix products, arithmetic and copies ran while one was open for 0% -> 0% of each run, Pallas kernels for 0% -> 0%
where the time goes in v2:
time: 55.2 us; the launch traced here: 55.1 us
  Pallas kernels  55.1 us (100%)
    pallas_call x1, Pallas kernels, grad_weights(): pl.pallas_call(functools.partial(comm_kernel, scale), out_shape=jax.Shape...  50.7 us
    pallas_call x1, Pallas kernels, symmetric_product(): pl.pallas_call(sum_kernel, out_shape=jax.ShapeDtypeStruct(shape, jnp.bflo...  4.37 us

profile of v2, /device:TPU:1, one launch (start us, length us, event | category | flops | bytes accessed | tf_op | source)
XLA Modules:
  0.0 55.1 jit_solution(3495714807387556562)
XLA Ops:
  0.0 0.0 copy-start
  0.0 50.7 %shard_map.28.g_ref = bf16[1024,1024]{1,0:T(8,128)(2,1)S(1)} custom-call(bf16[1024,1408]{1,0:T(8,128)(2,1)} %p_ref.1, bf16[4,1024]{1,0:T(4,128)(2,1)} %u_hbm.1), custom_call_target="tpu_custom_call" | custom-call | tf_op jit(solution)/shard_map/pallas_call | solution.py:468
  50.8 0.0 copy-done
  50.8 4.4 %shard_map.29 = bf16[1024,1408]{1,0:T(8,128)(2,1)} custom-call(bf16[1024,1024]{1,0:T(8,128)(2,1)S(1)} %shard_map.28.g_ref, bf16[1024,1408]{1,0:T(8,128)(2,1)S(1)} %copy-done), custom_call_target="tpu_custom_call" | custom-call | tf_op jit(solution)/shard_map/pallas_call | solution.py:452
Async XLA Ops:
  0.0 50.8 %copy-start = (bf16[1024,1408]{1,0:T(8,128)(2,1)S(1)}, bf16[1024,1408]{1,0:T(8,128)(2,1)}, u32[]{:S(2)}) copy-start(bf16[1024,1408]{1,0:T(8,128)(2,1)} %p_ref.1) | copy-start | bytes 8650756
